TPU v7x, 32 devices: a whole 2x2x4 slice. The times are simulated.
32 devices in a mesh: replica: 2 (over x), tp: 8 (over z, y), sub: 2 (over core).
Axes of the slice: x: 2, y: 2, z: 4, core: 2. Of those that a mesh axis runs over, the one named last changes fastest.
Arguments:
- hidden_in: bfloat16 [8, 8192], P('replica'), parts along dimension 0, may hold values from -6 to 6
- norm_gain: float32 [16384], P('replica'), parts along dimension 0, may hold values from 0.1 to 1.9
- wqkv_old: bfloat16 [16, 2, 1280, 4096], P(('replica', 'tp'), 'sub'), parts along dimension 0, may hold values from -0.1875 to 0.1875
- wo: bfloat16 [16384, 8192], P(('replica', 'tp', 'sub')), parts along dimension 0, may hold values from -0.0625 to 0.0625
- key_cache: bfloat16 [8, 4096, 1024], P('replica', ('tp', 'sub')), parts along dimension 0, may hold values from -240 to 240
- value_cache: bfloat16 [8, 4096, 1024], P('replica', ('tp', 'sub')), parts along dimension 0, may hold values from -6 to 6
- lengths: int32 [8], P('replica'), parts along dimension 0, may hold values from 1 to 4096
- section_order: int32 [32], P('replica'), parts along dimension 0, may hold values from 0 to 15, each once
Outputs:
- mixed_out: bfloat16 [8, 8192], P('replica'), parts along dimension 0
- wqkv_new: bfloat16 [16, 2, 640, 8192], P(('replica', 'tp'), 'sub'), parts along dimension 0
There are 2 independent parts, one for each index of `replica`. A program takes and returns all parts, laid end to end along the dimension named above; each array names one. Nothing has to cross between parts.
Inputs may be any that keep to these rules, and one draw needn't show every extreme that they name: `section_order`: each input row block appears once. The new token's position is lengths[b].
All inputs are finite; a program needn't handle non-finite values.
Results may differ from a plain program's by a relative error of at most 0.0085.
The roundings to bfloat16 on the way count: a program that leaves them out, or rounds other values in their place, can miss the bound.
Values may be sent and summed in bfloat16 or wider, within the bound.
A program may use at most 128 MiB of HBM per device.

v0:
```python
import math
import jax
import jax.numpy as jnp
from jax import lax
from jax.sharding import PartitionSpec as P

HEADS = 64
KV_HEADS = 8
HEAD_DIM = 128
RANKS = 8
ROW_BLOCKS = 16


def passed_along(value, axis, steps):
    count = lax.axis_size(axis)
    pairs = [(source, (source + steps) % count) for source in range(count)]
    return lax.ppermute(value, axis, pairs)


def rotary(values, positions):
    half = values.shape[-1] // 2
    freqs = 500000.0 ** (-jnp.arange(half, dtype=jnp.float32) * 2.0 / values.shape[-1])
    angles = positions.astype(jnp.float32)[:, None] * freqs[None, :]
    cosine = jnp.cos(angles)[:, None, :]
    sine = jnp.sin(angles)[:, None, :]
    first_half = values[..., :half]
    second_half = values[..., half:]
    return jnp.concatenate(
        [first_half * cosine - second_half * sine, second_half * cosine + first_half * sine], -1
    )


def rms_normed(hidden_in, norm_gain):
    widened = hidden_in.astype(jnp.float32)
    factor = lax.rsqrt(jnp.mean(widened * widened, -1, keepdims=True) + 1e-05)
    return (widened, (widened * factor * norm_gain).astype(jnp.bfloat16))


def shards(hidden_in, norm_gain, wqkv_old, wo, key_cache, value_cache, lengths, section_order):
    tp_count = lax.axis_size("tp")
    section_count = tp_count // 4
    per_section = ROW_BLOCKS // section_count
    tp_index = lax.axis_index("tp")
    sub_index = lax.axis_index("sub")
    own_section = tp_index // 4
    device_rank = tp_index * 2 + sub_index
    cols_dev = wqkv_old.shape[2] // section_count
    rows_old = wqkv_old.shape[3]
    block_rows = rows_old // per_section
    old_block = wqkv_old[0, 0].reshape(section_count, cols_dev, rows_old)
    slot_ids = jnp.arange(section_count, dtype=jnp.int32)
    arrived = [lax.dynamic_index_in_dim(old_block, own_section, 0, keepdims=False)]
    for offset in range(1, section_count):
        outgoing = lax.dynamic_index_in_dim(
            old_block, (own_section + offset) % section_count, 0, keepdims=False
        )
        arrived.append(passed_along(outgoing, "tp", 4 * offset))
    received = jnp.stack(arrived, 0)
    sources = (own_section - slot_ids) % section_count
    block_ids = jnp.arange(ROW_BLOCKS, dtype=jnp.int32)
    local_source = (
        sources[:, None] * per_section + jnp.arange(per_section, dtype=jnp.int32)[None, :]
    ).reshape(ROW_BLOCKS)
    target_block = jnp.take(section_order, local_source, axis=0)
    placing = (target_block[None, :] == block_ids[:, None]).astype(jnp.bfloat16)
    received_blocks = jnp.transpose(
        received.reshape(section_count, cols_dev, per_section, block_rows), (0, 2, 1, 3)
    ).reshape(ROW_BLOCKS, cols_dev, block_rows)
    new_weight = jnp.einsum(
        "sa,acr->csr", placing, received_blocks, preferred_element_type=jnp.float32
    ).astype(jnp.bfloat16)
    new_weight = new_weight.reshape(cols_dev, ROW_BLOCKS * block_rows)
    widened, normed = rms_normed(hidden_in, norm_gain)
    projected = lax.dot_general(
        normed, new_weight, (((1,), (1,)), ((), ())), preferred_element_type=jnp.float32
    ).astype(jnp.bfloat16)
    gathered = lax.all_gather(projected[:, None, :], ("tp", "sub"), axis=1, tiled=True)
    seq_count = hidden_in.shape[0]
    projected_all = jnp.transpose(
        gathered.reshape(seq_count, section_count, RANKS, cols_dev), (0, 2, 1, 3)
    ).reshape(seq_count, -1)
    q_width = HEADS * HEAD_DIM
    kv_width = KV_HEADS * HEAD_DIM
    groups = HEADS // KV_HEADS
    queries = rotary(
        projected_all[:, :q_width].astype(jnp.float32).reshape(seq_count, HEADS, HEAD_DIM), lengths
    ).astype(jnp.bfloat16)
    new_keys = rotary(
        projected_all[:, q_width : q_width + kv_width]
        .astype(jnp.float32)
        .reshape(seq_count, KV_HEADS, HEAD_DIM),
        lengths,
    ).astype(jnp.bfloat16)
    new_values = (
        projected_all[:, q_width + kv_width :]
        .astype(jnp.float32)
        .reshape(seq_count, KV_HEADS, HEAD_DIM)
    )
    pos_count = key_cache.shape[1]
    positions = device_rank * pos_count + jnp.arange(pos_count, dtype=jnp.int32)
    usable = (positions[None, :] < lengths[:, None])[:, None, None, :]
    inverse = 1.0 / math.sqrt(HEAD_DIM)
    grouped = queries.reshape(seq_count, KV_HEADS, groups, HEAD_DIM)
    keys_local = key_cache.reshape(seq_count, pos_count, KV_HEADS, HEAD_DIM)
    values_local = value_cache.reshape(seq_count, pos_count, KV_HEADS, HEAD_DIM).astype(jnp.float32)
    scores = (
        jnp.einsum("bkgd,bpkd->bkgp", grouped, keys_local, preferred_element_type=jnp.float32)
        * inverse
    )
    local_top = jnp.max(jnp.where(usable, scores, -1e30), -1)
    weights = jnp.exp(jnp.where(usable, scores - local_top[..., None], -1e30))
    local_sum = jnp.sum(weights, -1).reshape(seq_count, HEADS)
    local_mix = jnp.einsum("bkgp,bpkd->bkgd", weights, values_local).reshape(
        seq_count, HEADS, HEAD_DIM
    )
    local_top = local_top.reshape(seq_count, HEADS)
    heads_dev = wo.shape[0] // HEAD_DIM
    first_head = device_rank * heads_dev
    tops_in, sums_in, mixes_in = (
        lax.all_to_all(local_top[None], ("tp", "sub"), split_axis=2, concat_axis=0, tiled=True),
        lax.all_to_all(local_sum[None], ("tp", "sub"), split_axis=2, concat_axis=0, tiled=True),
        lax.all_to_all(local_mix[None], ("tp", "sub"), split_axis=2, concat_axis=0, tiled=True),
    )
    best = jnp.max(tops_in, 0)
    factors = jnp.exp(tops_in - best[None])
    head_sum = jnp.sum(sums_in * factors, 0)
    head_mix = jnp.sum(mixes_in * factors[..., None], 0)
    own_queries = lax.dynamic_slice_in_dim(queries, first_head, heads_dev, 1).astype(jnp.float32)
    kv_index = (first_head + jnp.arange(heads_dev, dtype=jnp.int32)) // groups
    own_keys = jnp.take(new_keys, kv_index, axis=1).astype(jnp.float32)
    own_values = jnp.take(new_values, kv_index, axis=1)
    own_score = jnp.sum(own_queries * own_keys, -1) * inverse
    highest = jnp.maximum(best, own_score)
    old_scale = jnp.exp(best - highest)
    own_weight = jnp.exp(own_score - highest)
    numerator = head_mix * old_scale[..., None] + own_weight[..., None] * own_values
    denominator = head_sum * old_scale + own_weight
    attended = (
        (numerator / denominator[..., None])
        .reshape(seq_count, heads_dev * HEAD_DIM)
        .astype(jnp.bfloat16)
    )
    partial_out = jnp.dot(attended, wo, preferred_element_type=jnp.float32)
    summed_out = lax.psum(partial_out, ("tp", "sub"))
    mixed_out = (widened + summed_out).astype(jnp.bfloat16)
    return (mixed_out, new_weight[None, None])


def solution(mesh):
    placed = (
        P("replica", None),
        P("replica"),
        P(("replica", "tp"), "sub", None, None),
        P(("replica", "tp", "sub"), None),
        P("replica", ("tp", "sub"), None),
        P("replica", ("tp", "sub"), None),
        P("replica"),
        P("replica"),
    )
    return jax.shard_map(
        shards,
        mesh=mesh,
        in_specs=placed,
        out_specs=(P("replica", None), P(("replica", "tp"), "sub", None, None)),
        check_vma=False,
    )
```

profile of v0, /device:TPU:8, one launch (start us, length us, event | category | flops | bytes accessed | tf_op | source)
XLA Modules:
  0.0 444.4 jit_solution(11691780571699023312)
XLA Ops:
  7.2 9.9 %constant_dynamic-slice_fusion = (bf16[1,640,4096]{2,1,0:T(8,128)(2,1)}, bf16[640,4096]{1,0:T(8,128)(2,1)}) fusion(bf16[2,640,4096]{2,1,0:T(8,128)(2,1)} %bitcast.145, s32[]{:T(128)S(6)} %select_n.109, s32[]{:T(128)S(6)} %select_n.111), kind=kLoop, calls=%fused_computation.104 | loop fusion | bytes 20971528 | tf_op jit(solution)/shard_map/jit(dynamic_index_in_dim)/dynamic_slice | solution.py:52
  17.1 2.6 collective-permute-start
  19.9 8.3 %copy.49 = bf16[80,8,8,512]{3,2,1,0:T(8,128)(2,1)} copy(bf16[80,8,8,512]{3,1,2,0:T(8,128)(2,1)} %bitcast.144) | data formatting | bytes 10485760
  29.5 215.0 %collective-permute-done = bf16[640,4096]{1,0:T(8,128)(2,1)} collective-permute-done((bf16[640,4096]{1,0:T(8,128)(2,1)}, bf16[640,4096]{1,0:T(8,128)(2,1)}, u32[]{:S(2)}, u32[]{:S(2)}) %collective-permute-start) | collective-permute-done | bytes 5242912 | tf_op jit(solution)/shard_map/ppermute | solution.py:17
  244.5 6.1 %copy.50 = bf16[80,8,8,512]{3,2,1,0:T(8,128)(2,1)S(1)} copy(bf16[80,8,8,512]{3,1,2,0:T(8,128)(2,1)} %bitcast.49) | data formatting | bytes 10485760
  250.7 5.6 %fusion.3 = bf16[640,512,16]{1,2,0:T(8,128)(2,1)} fusion(bf16[1,640,8,512]{3,2,0,1:T(8,128)(2,1)S(1)} %bitcast.149, bf16[1,640,8,512]{3,2,0,1:T(8,128)(2,1)S(1)} %bitcast.148, s32[16]{0:T(128)S(1)} %and_select_fusion.2), kind=kOutput, calls=%fused_computation.7 | convolution fusion | flops 178258176 | bytes 20971584 | tf_op jit(solution)/shard_map/sa,acr->csr/dot_general | solution.py:69
  256.3 20.5 %copy.51 = bf16[80,8,16,512]{3,1,2,0:T(8,128)(2,1)} copy(bf16[80,8,16,512]{3,2,1,0:T(8,128)(2,1)} %bitcast.141) | data formatting | bytes 20971520
  276.8 6.8 %convolution_convert_fusion = bf16[4,640]{1,0:T(4,128)(2,1)S(1)} fusion(bf16[640,8192]{1,0:T(8,128)(2,1)} %bitcast.143, bf16[4,8192]{1,0:T(4,128)(2,1)S(1)} %copy-done.2, f32[8192]{0:T(1024)S(1)} %copy-done.3, f32[4]{0:T(128)S(1)} %add_rsqrt_fusion), kind=kOutput, calls=%fused_computation.17 | convolution fusion | flops 42076672 | bytes 10589200 | tf_op jit(solution)/shard_map/dot_general | solution.py:74
  283.6 19.8 %all-gather = bf16[4,10240]{1,0:T(4,128)(2,1)S(1)} all-gather(bf16[4,640]{1,0:T(4,128)(2,1)S(1)} %convolution_convert_fusion), channel_id=2, replica_groups=mesh['replica'=2,'tp'=8,'sub'=2] {'tp','sub'}, dimensions={1}, use_global_device_ids=true | all-gather | bytes 87040 | tf_op jit(solution)/shard_map/all_gather | solution.py:77
  303.8 0.8 select_reduce_fusion
  304.8 2.0 fusion.13
  306.8 0.7 copy.45
  307.6 6.6 %all-to-all-start.2 = ((f32[1,4,64]{1,0,2:T(1,128)}), f32[1,4,64]{1,0,2:T(1,128)S(1)}, u32[]{:S(2)}, u32[]{:S(2)}) async-start(f32[1,4,64]{1,0,2:T(1,128)} %bitcast.29), calls=%async_computation.2 | async-start | bytes 65536 | tf_op jit(solution)/shard_map/all_to_all | solution.py:121
  314.3 0.7 copy.37
  315.6 3.6 all-to-all-done.2
  319.3 5.0 %all-to-all-start.1 = ((f32[1,4,64]{1,0,2:T(1,128)}), f32[1,4,64]{1,0,2:T(1,128)S(1)}, u32[]{:S(2)}, u32[]{:S(2)}) async-start(f32[1,4,64]{1,0,2:T(1,128)} %bitcast.16), calls=%async_computation.1 | async-start | bytes 65536 | tf_op jit(solution)/shard_map/all_to_all | solution.py:120
  324.4 0.7 copy.36
  326.0 3.3 all-to-all-done.1
  329.4 5.0 %all-to-all-start = ((f32[1,4,64,128]{3,1,0,2:T(4,128)}), f32[1,4,64,128]{3,1,0,2:T(4,128)S(1)}, u32[]{:S(2)}, u32[]{:S(2)}) async-start(f32[1,4,64,128]{3,1,0,2:T(4,128)} %copy.36), calls=%async_computation | async-start | bytes 262144 | tf_op jit(solution)/shard_map/all_to_all | solution.py:122
  335.1 4.7 %all-to-all-done = f32[1,4,64,128]{3,1,0,2:T(4,128)S(1)} async-done(((f32[1,4,64,128]{3,1,0,2:T(4,128)}), f32[1,4,64,128]{3,1,0,2:T(4,128)S(1)}, u32[]{:S(2)}, u32[]{:S(2)}) %all-to-all-start) | async-done | bytes 131104 | tf_op jit(solution)/shard_map/all_to_all | solution.py:122
  339.9 5.3 %fusion.41 = f32[4,8192]{1,0:T(4,128)} fusion(bf16[512,8192]{1,0:T(8,128)(2,1)} %param.11, f32[1,4,4,128]{3,2,1,0:T(4,128)S(1)} %broadcast_bitcast_fusion, f32[4,4,128]{2,1,0:T(4,128)S(1)} %gather_fusion.2, f32[1,4,4,128]{3,2,1,0:T(4,128)S(1)} %broadcast_bitcast_fusion.1, f32[4,4,128]{2,0,1:T(4,128)S(1)} %multiply_reduce_fusion, f32[4,4]{0,1:T(4,128)S(1)} %copy.41, ...), kind=kOutput, calls=%fused_computation.69 | convolution fusion | flops 33566720 | bytes 8553024 | tf_op jit(solution)/shard_map/dot_general | solution.py:143
  345.2 16.5 %broadcast_in_dim_reshape.15 = bf16[1,1,640,8192]{3,2,1,0:T(8,128)(2,1)} reshape(bf16[640,16,512]{2,1,0:T(8,128)(2,1)} %bitcast.142) | data formatting | bytes 20971520 | tf_op jit(solution)/shard_map/broadcast_in_dim;reshape | solution.py:146
  361.7 74.2 %all-reduce.2.cloned.1.call-done = f32[4,8192]{1,0:T(4,128)} async-done(((f32[4,8192]{1,0:T(4,128)}), f32[4,8192]{1,0:T(4,128)}) %all-reduce.2.cloned.1.call-update) | async-done | bytes 131088 | tf_op jit(solution)/shard_map/psum | solution.py:144
  435.9 1.6 fusion.20
  (60 shorter events, 4.7 us)
Async XLA Ops:
  7.2 296.6 %copy-start = (bf16[4,256,1024]{2,1,0:T(8,128)(2,1)S(1)}, bf16[4,256,1024]{2,1,0:T(8,128)(2,1)}, u32[]{:S(2)}) copy-start(bf16[4,256,1024]{2,1,0:T(8,128)(2,1)} %param.12) | copy-start | bytes 6291460
  17.1 227.4 %collective-permute-start = (bf16[640,4096]{1,0:T(8,128)(2,1)}, bf16[640,4096]{1,0:T(8,128)(2,1)}, u32[]{:S(2)}, u32[]{:S(2)}) collective-permute-start(bf16[640,4096]{1,0:T(8,128)(2,1)} %get-tuple-element.8), channel_id=1, source_target_pairs={{0,8},{2,10},{4,12},{6,14},{8,0},{10,2},{12,4},{14,6},{1,9},{3,11}... | collective-permute-start | bytes 15728648 | tf_op jit(solution)/shard_map/ppermute | solution.py:17
  19.9 8.4 %copy-start.4 = (s32[4]{0:T(128)S(1)}, s32[4]{0:T(128)}, u32[]{:S(2)}) copy-start(s32[4]{0:T(128)} %param.14) | copy-start | bytes 52
  19.9 8.4 %copy-start.1 = (s32[16]{0:T(128)S(1)}, s32[16]{0:T(128)}, u32[]{:S(2)}) copy-start(s32[16]{0:T(128)} %param.15) | copy-start | bytes 196
  19.9 9.1 %copy-start.2 = (bf16[4,8192]{1,0:T(4,128)(2,1)S(1)}, bf16[4,8192]{1,0:T(4,128)(2,1)}, u32[]{:S(2)}) copy-start(bf16[4,8192]{1,0:T(4,128)(2,1)} %param.8) | copy-start | bytes 196612
  28.3 222.4 %slice-start = ((s8[5242880]{0:T(1024)(128)(4,1)}), s8[1048576]{0:T(1024)(128)(4,1)S(1)}, s32[]{:S(2)}) async-start(s8[5242880]{0:T(1024)(128)(4,1)} %bitcast.146), calls=%async_computation.4 | async-start | bytes 2097152
  244.5 6.1 %slice-start.1 = ((s8[5242880]{0:T(1024)(128)(4,1)}), s8[4194304]{0:T(1024)(128)(4,1)S(1)}, s32[]{:S(2)}) async-start(s8[5242880]{0:T(1024)(128)(4,1)} %bitcast.146), calls=%async_computation.5 | async-start | bytes 8388608
  256.3 20.6 %copy-start.3 = (f32[8192]{0:T(1024)S(1)}, f32[8192]{0:T(1024)}, u32[]{:S(2)}) copy-start(f32[8192]{0:T(1024)} %param.9) | copy-start | bytes 98308
  307.6 11.7 %all-to-all-start.2 = ((f32[1,4,64]{1,0,2:T(1,128)}), f32[1,4,64]{1,0,2:T(1,128)S(1)}, u32[]{:S(2)}, u32[]{:S(2)}) async-start(f32[1,4,64]{1,0,2:T(1,128)} %bitcast.29), calls=%async_computation.2 | async-start | bytes 65536 | tf_op jit(solution)/shard_map/all_to_all | solution.py:121
  319.3 10.1 %all-to-all-start.1 = ((f32[1,4,64]{1,0,2:T(1,128)}), f32[1,4,64]{1,0,2:T(1,128)S(1)}, u32[]{:S(2)}, u32[]{:S(2)}) async-start(f32[1,4,64]{1,0,2:T(1,128)} %bitcast.16), calls=%async_computation.1 | async-start | bytes 65536 | tf_op jit(solution)/shard_map/all_to_all | solution.py:120
  329.4 10.4 %all-to-all-start = ((f32[1,4,64,128]{3,1,0,2:T(4,128)}), f32[1,4,64,128]{3,1,0,2:T(4,128)S(1)}, u32[]{:S(2)}, u32[]{:S(2)}) async-start(f32[1,4,64,128]{3,1,0,2:T(4,128)} %copy.36), calls=%async_computation | async-start | bytes 262144 | tf_op jit(solution)/shard_map/all_to_all | solution.py:122
  334.4 101.6 %all-reduce.2.cloned.1.call-start = ((), (), s32[]{:S(2)}) async-start(), calls=%async_computation.3 | async-start | bytes 262144 | tf_op jit(solution)/shard_map/psum | solution.py:144
Sparse Core Ops, SparseCore 0:
  345.4 90.5 all-reduce.1
where the time goes:
time: 445 us; the launch traced here: 444 us
  waiting for transfers between devices  301 us (68%)
  local copies, waits for them, and re-layouts  66.7 us (15%)
  matrix products  20.4 us (5%)
  blocking collectives  19.8 us (4%)
  starting transfers between devices  19.2 us (4%)
  between operations  14.3 us (3%)
    ppermute x1, waiting for transfers between devices, passed_along(): return lax.ppermute(value, axis, pairs)  215 us
    psum x1, waiting for transfers between devices, shards(): summed_out = lax.psum(partial_out, ('tp', 'sub'))  74.2 us
    unnamed x20, local copies, waits for them, and re-layouts  35.2 us
    all_gather x1, blocking collectives, shards(): lax.all_gather(projected[:, None, :], ('tp', 'sub'), axis=1, tiled=True)  19.8 us
    another operation x1, local copies, waits for them, and re-layouts, shards(): return (mixed_out, new_weight[None, None])  16.5 us
    dynamic_slice x1, local copies, waits for them, and re-layouts, shards(): lax.dynamic_index_in_dim(old_block, own_section, 0, keepdims=False)  9.85 us
  transfers between devices with their start and end apart: 5, of which 5 were waited for; matrix products, arithmetic and copies ran while one was open for 7% of the time, Pallas kernels for 0%

commit v1 on v0

--- a/solution.py
+++ b/solution.py
@@ -141,7 +141,7 @@
         .astype(jnp.bfloat16)
     )
     partial_out = jnp.dot(attended, wo, preferred_element_type=jnp.float32)
-    summed_out = lax.psum(partial_out, ("tp", "sub"))
+    summed_out = lax.psum(lax.psum(partial_out, "sub"), "tp")
     mixed_out = (widened + summed_out).astype(jnp.bfloat16)
     return (mixed_out, new_weight[None, None])
 

time: 445 us -> 449 us (level)
    psum x1 -> x2, waiting for transfers between devices: 74.2 us -> 75.7 us  [shards(): summed_out = lax.psum(lax.psum(partial_out, 'sub'), 'tp')]
  transfers between devices with their start and end apart: 5 -> 6, of which waited for: 5 -> 6; matrix products, arithmetic and copies ran while one was open for 7% -> 7% of each run, Pallas kernels for 0% -> 0%
where the time goes in v1:
time: 449 us; the launch traced here: 446 us
  waiting for transfers between devices  302 us (67%)
  local copies, waits for them, and re-layouts  66.7 us (15%)
  matrix products  20.4 us (5%)
  blocking collectives  19.8 us (4%)
  starting transfers between devices  19.2 us (4%)
  between operations  14.3 us (3%)
    ppermute x1, waiting for transfers between devices, passed_along(): return lax.ppermute(value, axis, pairs)  215 us
    psum x2, waiting for transfers between devices, shards(): summed_out = lax.psum(lax.psum(partial_out, 'sub'), 'tp')  75.7 us
    unnamed x20, local copies, waits for them, and re-layouts  35.2 us
    all_gather x1, blocking collectives, shards(): lax.all_gather(projected[:, None, :], ('tp', 'sub'), axis=1, tiled=True)  19.8 us
    another operation x1, local copies, waits for them, and re-layouts, shards(): return (mixed_out, new_weight[None, None])  16.5 us
    dynamic_slice x1, local copies, waits for them, and re-layouts, shards(): lax.dynamic_index_in_dim(old_block, own_section, 0, keepdims=False)  9.85 us
  transfers between devices with their start and end apart: 6, of which 6 were waited for; matrix products, arithmetic and copies ran while one was open for 7% of the time, Pallas kernels for 0%

profile of v1, /device:TPU:8, one launch (start us, length us, event | category | flops | bytes accessed | tf_op | source)
XLA Modules:
  0.0 445.9 jit_solution(4047615582670502365)
XLA Ops:
  7.2 9.9 %constant_dynamic-slice_fusion = (bf16[1,640,4096]{2,1,0:T(8,128)(2,1)}, bf16[640,4096]{1,0:T(8,128)(2,1)}) fusion(bf16[2,640,4096]{2,1,0:T(8,128)(2,1)} %bitcast.145, s32[]{:T(128)S(6)} %select_n.109, s32[]{:T(128)S(6)} %select_n.111), kind=kLoop, calls=%fused_computation.104 | loop fusion | bytes 20971528 | tf_op jit(solution)/shard_map/jit(dynamic_index_in_dim)/dynamic_slice | solution.py:52
  17.1 2.6 collective-permute-start
  19.9 8.3 %copy.49 = bf16[80,8,8,512]{3,2,1,0:T(8,128)(2,1)} copy(bf16[80,8,8,512]{3,1,2,0:T(8,128)(2,1)} %bitcast.144) | data formatting | bytes 10485760
  29.5 215.0 %collective-permute-done = bf16[640,4096]{1,0:T(8,128)(2,1)} collective-permute-done((bf16[640,4096]{1,0:T(8,128)(2,1)}, bf16[640,4096]{1,0:T(8,128)(2,1)}, u32[]{:S(2)}, u32[]{:S(2)}) %collective-permute-start) | collective-permute-done | bytes 5242912 | tf_op jit(solution)/shard_map/ppermute | solution.py:17
  244.5 6.1 %copy.50 = bf16[80,8,8,512]{3,2,1,0:T(8,128)(2,1)S(1)} copy(bf16[80,8,8,512]{3,1,2,0:T(8,128)(2,1)} %bitcast.49) | data formatting | bytes 10485760
  250.7 5.6 %fusion.3 = bf16[640,512,16]{1,2,0:T(8,128)(2,1)} fusion(bf16[1,640,8,512]{3,2,0,1:T(8,128)(2,1)S(1)} %bitcast.149, bf16[1,640,8,512]{3,2,0,1:T(8,128)(2,1)S(1)} %bitcast.148, s32[16]{0:T(128)S(1)} %and_select_fusion.2), kind=kOutput, calls=%fused_computation.7 | convolution fusion | flops 178258176 | bytes 20971584 | tf_op jit(solution)/shard_map/sa,acr->csr/dot_general | solution.py:69
  256.3 20.5 %copy.51 = bf16[80,8,16,512]{3,1,2,0:T(8,128)(2,1)} copy(bf16[80,8,16,512]{3,2,1,0:T(8,128)(2,1)} %bitcast.141) | data formatting | bytes 20971520
  276.8 6.8 %convolution_convert_fusion = bf16[4,640]{1,0:T(4,128)(2,1)S(1)} fusion(bf16[640,8192]{1,0:T(8,128)(2,1)} %bitcast.143, bf16[4,8192]{1,0:T(4,128)(2,1)S(1)} %copy-done.2, f32[8192]{0:T(1024)S(1)} %copy-done.3, f32[4]{0:T(128)S(1)} %add_rsqrt_fusion), kind=kOutput, calls=%fused_computation.17 | convolution fusion | flops 42076672 | bytes 10589200 | tf_op jit(solution)/shard_map/dot_general | solution.py:74
  283.6 19.8 %all-gather = bf16[4,10240]{1,0:T(4,128)(2,1)S(1)} all-gather(bf16[4,640]{1,0:T(4,128)(2,1)S(1)} %convolution_convert_fusion), channel_id=2, replica_groups=mesh['replica'=2,'tp'=8,'sub'=2] {'tp','sub'}, dimensions={1}, use_global_device_ids=true | all-gather | bytes 87040 | tf_op jit(solution)/shard_map/all_gather | solution.py:77
  303.8 0.8 select_reduce_fusion
  304.8 2.0 fusion.13
  306.8 0.7 copy.45
  307.6 6.6 %all-to-all-start.2 = ((f32[1,4,64]{1,0,2:T(1,128)}), f32[1,4,64]{1,0,2:T(1,128)S(1)}, u32[]{:S(2)}, u32[]{:S(2)}) async-start(f32[1,4,64]{1,0,2:T(1,128)} %bitcast.29), calls=%async_computation.2 | async-start | bytes 65536 | tf_op jit(solution)/shard_map/all_to_all | solution.py:121
  315.6 3.6 all-to-all-done.2
  319.3 5.0 %all-to-all-start.1 = ((f32[1,4,64]{1,0,2:T(1,128)}), f32[1,4,64]{1,0,2:T(1,128)S(1)}, u32[]{:S(2)}, u32[]{:S(2)}) async-start(f32[1,4,64]{1,0,2:T(1,128)} %bitcast.16), calls=%async_computation.1 | async-start | bytes 65536 | tf_op jit(solution)/shard_map/all_to_all | solution.py:120
  324.4 0.7 copy.36
  326.0 3.3 all-to-all-done.1
  329.4 5.0 %all-to-all-start = ((f32[1,4,64,128]{3,1,0,2:T(4,128)}), f32[1,4,64,128]{3,1,0,2:T(4,128)S(1)}, u32[]{:S(2)}, u32[]{:S(2)}) async-start(f32[1,4,64,128]{3,1,0,2:T(4,128)} %copy.36), calls=%async_computation | async-start | bytes 262144 | tf_op jit(solution)/shard_map/all_to_all | solution.py:122
  335.1 4.6 %all-to-all-done = f32[1,4,64,128]{3,1,0,2:T(4,128)S(1)} async-done(((f32[1,4,64,128]{3,1,0,2:T(4,128)}), f32[1,4,64,128]{3,1,0,2:T(4,128)S(1)}, u32[]{:S(2)}, u32[]{:S(2)}) %all-to-all-start) | async-done | bytes 131104 | tf_op jit(solution)/shard_map/all_to_all | solution.py:122
  339.9 5.3 %fusion.41 = f32[4,8192]{1,0:T(4,128)} fusion(bf16[512,8192]{1,0:T(8,128)(2,1)} %param.11, f32[1,4,4,128]{3,2,1,0:T(4,128)S(1)} %broadcast_bitcast_fusion, f32[4,4,128]{2,1,0:T(4,128)S(1)} %gather_fusion.2, f32[1,4,4,128]{3,2,1,0:T(4,128)S(1)} %broadcast_bitcast_fusion.1, f32[4,4,128]{2,0,1:T(4,128)S(1)} %multiply_reduce_fusion, f32[4,4]{0,1:T(4,128)S(1)} %copy.41, ...), kind=kOutput, calls=%fused_computation.69 | convolution fusion | flops 33566720 | bytes 8553024 | tf_op jit(solution)/shard_map/dot_general | solution.py:143
  345.3 18.1 %all-reduce.3.cloned.1.call-done = f32[4,8192]{1,0:T(4,128)} async-done(((f32[4,8192]{1,0:T(4,128)}), f32[4,8192]{1,0:T(4,128)}) %all-reduce.3.cloned.1.call-update) | async-done | bytes 131088 | tf_op jit(solution)/shard_map/psum | solution.py:144
  363.4 16.5 %broadcast_in_dim_reshape.15 = bf16[1,1,640,8192]{3,2,1,0:T(8,128)(2,1)} reshape(bf16[640,16,512]{2,1,0:T(8,128)(2,1)} %bitcast.142) | data formatting | bytes 20971520 | tf_op jit(solution)/shard_map/broadcast_in_dim;reshape | solution.py:146
  379.9 57.6 %all-reduce.5.cloned.1.call-done = f32[4,8192]{1,0:T(4,128)} async-done(((f32[4,8192]{1,0:T(4,128)}), f32[4,8192]{1,0:T(4,128)}) %all-reduce.5.cloned.1.call-update) | async-done | bytes 131088 | tf_op jit(solution)/shard_map/psum | solution.py:144
  437.5 1.6 fusion.20
  (63 shorter events, 5.5 us)
Async XLA Ops:
  7.2 296.6 %copy-start = (bf16[4,256,1024]{2,1,0:T(8,128)(2,1)S(1)}, bf16[4,256,1024]{2,1,0:T(8,128)(2,1)}, u32[]{:S(2)}) copy-start(bf16[4,256,1024]{2,1,0:T(8,128)(2,1)} %param.12) | copy-start | bytes 6291460
  17.1 227.4 %collective-permute-start = (bf16[640,4096]{1,0:T(8,128)(2,1)}, bf16[640,4096]{1,0:T(8,128)(2,1)}, u32[]{:S(2)}, u32[]{:S(2)}) collective-permute-start(bf16[640,4096]{1,0:T(8,128)(2,1)} %get-tuple-element.8), channel_id=1, source_target_pairs={{0,8},{2,10},{4,12},{6,14},{8,0},{10,2},{12,4},{14,6},{1,9},{3,11}... | collective-permute-start | bytes 15728648 | tf_op jit(solution)/shard_map/ppermute | solution.py:17
  19.9 8.4 %copy-start.4 = (s32[4]{0:T(128)S(1)}, s32[4]{0:T(128)}, u32[]{:S(2)}) copy-start(s32[4]{0:T(128)} %param.14) | copy-start | bytes 52
  19.9 8.4 %copy-start.1 = (s32[16]{0:T(128)S(1)}, s32[16]{0:T(128)}, u32[]{:S(2)}) copy-start(s32[16]{0:T(128)} %param.15) | copy-start | bytes 196
  19.9 9.1 %copy-start.2 = (bf16[4,8192]{1,0:T(4,128)(2,1)S(1)}, bf16[4,8192]{1,0:T(4,128)(2,1)}, u32[]{:S(2)}) copy-start(bf16[4,8192]{1,0:T(4,128)(2,1)} %param.8) | copy-start | bytes 196612
  28.3 222.4 %slice-start = ((s8[5242880]{0:T(1024)(128)(4,1)}), s8[1048576]{0:T(1024)(128)(4,1)S(1)}, s32[]{:S(2)}) async-start(s8[5242880]{0:T(1024)(128)(4,1)} %bitcast.146), calls=%async_computation.5 | async-start | bytes 2097152
  244.5 6.1 %slice-start.1 = ((s8[5242880]{0:T(1024)(128)(4,1)}), s8[4194304]{0:T(1024)(128)(4,1)S(1)}, s32[]{:S(2)}) async-start(s8[5242880]{0:T(1024)(128)(4,1)} %bitcast.146), calls=%async_computation.6 | async-start | bytes 8388608
  256.3 20.6 %copy-start.3 = (f32[8192]{0:T(1024)S(1)}, f32[8192]{0:T(1024)}, u32[]{:S(2)}) copy-start(f32[8192]{0:T(1024)} %param.9) | copy-start | bytes 98308
  307.6 11.7 %all-to-all-start.2 = ((f32[1,4,64]{1,0,2:T(1,128)}), f32[1,4,64]{1,0,2:T(1,128)S(1)}, u32[]{:S(2)}, u32[]{:S(2)}) async-start(f32[1,4,64]{1,0,2:T(1,128)} %bitcast.29), calls=%async_computation.2 | async-start | bytes 65536 | tf_op jit(solution)/shard_map/all_to_all | solution.py:121
  319.3 10.1 %all-to-all-start.1 = ((f32[1,4,64]{1,0,2:T(1,128)}), f32[1,4,64]{1,0,2:T(1,128)S(1)}, u32[]{:S(2)}, u32[]{:S(2)}) async-start(f32[1,4,64]{1,0,2:T(1,128)} %bitcast.16), calls=%async_computation.1 | async-start | bytes 65536 | tf_op jit(solution)/shard_map/all_to_all | solution.py:120
  329.4 10.4 %all-to-all-start = ((f32[1,4,64,128]{3,1,0,2:T(4,128)}), f32[1,4,64,128]{3,1,0,2:T(4,128)S(1)}, u32[]{:S(2)}, u32[]{:S(2)}) async-start(f32[1,4,64,128]{3,1,0,2:T(4,128)} %copy.36), calls=%async_computation | async-start | bytes 262144 | tf_op jit(solution)/shard_map/all_to_all | solution.py:122
  334.4 29.0 %all-reduce.3.cloned.1.call-start = ((), (), s32[]{:S(2)}) async-start(), calls=%async_computation.3 | async-start | bytes 262144 | tf_op jit(solution)/shard_map/psum | solution.py:144
  345.2 92.2 %all-reduce.5.cloned.1.call-start = ((), (), s32[]{:S(2)}) async-start(), calls=%async_computation.4 | async-start | bytes 262144 | tf_op jit(solution)/shard_map/psum | solution.py:144
Sparse Core Ops, SparseCore 0:
  345.4 18.0 all-reduce.2
  366.8 70.6 all-reduce.4
